TPU v7x, 32 devices: a whole 2x2x4 slice. The times are simulated.
32 devices in a mesh: section: 2 (over core), vocab: 16 (over z, y, x).
Axes of the slice: x: 2, y: 2, z: 4, core: 2. Of those that a mesh axis runs over, the one named last changes fastest.
Arguments:
- hidden_in: bfloat16 [2, 256, 7168], P(None, ('section', 'vocab')), may hold values from -6 to 6
- gain_ffn: float32 [7168], replicated, may hold values from 0.4 to 1.6
- w_gate: bfloat16 [7168, 18432], P(None, ('section', 'vocab')), may hold values from -0.0625 to 0.0625
- w_up: bfloat16 [7168, 18432], P(None, ('section', 'vocab')), may hold values from -0.0625 to 0.0625
- w_down: bfloat16 [18432, 7168], P(('section', 'vocab')), may hold values from -0.046875 to 0.046875
- gain_final: float32 [7168], replicated, may hold values from 0.4 to 1.6
- head_weight: bfloat16 [7168, 129280], P(None, ('section', 'vocab')), may hold values from -4.5 to 4.5
- sampled_ids: int32 [2, 256], replicated, may hold values from 0 to 129279
- seq_ids: int32 [2, 256], P(None, ('section', 'vocab')), may hold values from 0 to 7, never falling along the last dimension, each value on 1 to 128 neighbouring positions
Outputs:
- token_logprob: float32 [2, 256], P(None, ('section', 'vocab'))
- log_norm: float32 [2, 256], P(None, ('section', 'vocab'))
- top_mass: float32 [2, 256], P(None, ('section', 'vocab'))
- seq_logprob: float32 [2, 8], replicated
All inputs are finite; a program needn't handle non-finite values.
Results may differ from a plain program's by a relative error of at most 0.006.
Values may be sent and summed in bfloat16 or wider, within the bound.
No kernel may reach another device: no remote copies, remote signals or barrier semaphores. Data moves between devices by JAX's collectives and lax.ppermute only.
A program may use at most 192 MiB of HBM per device.

v0:
```python
import jax
import jax.numpy as jnp
from jax import lax
from jax.sharding import PartitionSpec as P

SEQS = 8
TOPK = 20
epsilon = 1e-06


def rms_norm(values, scale_gain):
    wide = values.astype(jnp.float32)
    square_mean = jnp.mean(wide * wide, axis=-1, keepdims=True)
    return (wide * lax.rsqrt(square_mean + epsilon) * scale_gain).astype(jnp.bfloat16)


def largest(values):
    return lax.sort(values, dimension=values.ndim - 1)[..., -TOPK:]


def finish(peak_value, sum_total, sampled_logit, leaders_all):
    log_norm = peak_value + jnp.log(sum_total)
    top_mass = jnp.sum(jnp.exp(leaders_all - log_norm[:, None]), axis=1)
    return (sampled_logit - log_norm, log_norm, top_mass)


def combine_sources(pieces):
    maxima, exp_sums, sampled_parts, top_values = pieces
    peak_value = jnp.max(maxima, axis=0)
    sum_total = jnp.sum(exp_sums * jnp.exp(maxima - peak_value[None, :]), axis=0)
    sampled_logit = jnp.sum(sampled_parts, axis=0)
    item_count = top_values.shape[1]
    pooled = jnp.transpose(top_values, (1, 0, 2)).reshape(item_count, -1)
    leaders_all = largest(pooled)
    return finish(peak_value, sum_total, sampled_logit, leaders_all)


def body(hidden_in, gain_ffn, w_gate, w_up, w_down, gain_final, head_weight, sampled_ids, seq_ids):
    row_count = hidden_in.shape[1]
    shard_width = head_weight.shape[1]
    position = lax.axis_index(("section", "vocab"))
    group_count = lax.axis_size(("section", "vocab"))
    columns = lax.broadcasted_iota(jnp.int32, (1, shard_width), 1) + position * shard_width
    logprob_list = []
    norm_list = []
    mass_list = []
    partials = []
    for microbatch in range(hidden_in.shape[0]):
        own_rows = hidden_in[microbatch]
        gathered = lax.all_gather(own_rows, ("section", "vocab"), axis=0, tiled=True)
        normed = rms_norm(gathered, gain_ffn)
        gate_proj = jnp.dot(normed, w_gate, preferred_element_type=jnp.float32)
        up_proj = jnp.dot(normed, w_up, preferred_element_type=jnp.float32)
        hidden_act = (jax.nn.silu(gate_proj) * up_proj).astype(jnp.bfloat16)
        branch = lax.psum(
            jnp.dot(hidden_act, w_down, preferred_element_type=jnp.float32), ("section", "vocab")
        )
        residual = (gathered.astype(jnp.float32) + branch).astype(jnp.bfloat16)
        scaled = rms_norm(residual, gain_final)
        logits = jnp.dot(scaled, head_weight, preferred_element_type=jnp.float32)
        token_ids = sampled_ids[microbatch]
        matches = columns == token_ids[:, None]
        sampled_part = jnp.sum(jnp.where(matches, logits, 0.0), axis=1)
        leaders = largest(logits)
        local_peak = jnp.max(logits, axis=1).reshape(group_count, row_count)
        local_total = jnp.sum(jnp.exp(logits - jnp.max(logits, axis=1)[:, None]), axis=1).reshape(
            group_count, row_count
        )
        sampled_block = sampled_part.reshape(group_count, row_count)
        leader_block = leaders.reshape(group_count, row_count, TOPK)
        token_logprob, log_norm, top_mass = combine_sources(
            (
                lax.all_to_all(
                    local_peak, ("section", "vocab"), split_axis=0, concat_axis=0, tiled=True
                ),
                lax.all_to_all(
                    local_total, ("section", "vocab"), split_axis=0, concat_axis=0, tiled=True
                ),
                lax.all_to_all(
                    sampled_block, ("section", "vocab"), split_axis=0, concat_axis=0, tiled=True
                ),
                lax.all_to_all(
                    leader_block, ("section", "vocab"), split_axis=0, concat_axis=0, tiled=True
                ),
            )
        )
        onehot = (
            seq_ids[microbatch][:, None] == jnp.arange(SEQS, dtype=jnp.int32)[None, :]
        ).astype(jnp.float32)
        partials.append(jnp.sum(token_logprob[:, None] * onehot, axis=0))
        logprob_list.append(token_logprob)
        norm_list.append(log_norm)
        mass_list.append(top_mass)
    seq_logprob = lax.psum(jnp.stack(partials), ("section", "vocab"))
    return (jnp.stack(logprob_list), jnp.stack(norm_list), jnp.stack(mass_list), seq_logprob)


def solution(mesh):
    in_specs = (
        P(None, ("section", "vocab"), None),
        P(),
        P(None, ("section", "vocab")),
        P(None, ("section", "vocab")),
        P(("section", "vocab"), None),
        P(),
        P(None, ("section", "vocab")),
        P(),
        P(None, ("section", "vocab")),
    )
    out_specs = (
        P(None, ("section", "vocab")),
        P(None, ("section", "vocab")),
        P(None, ("section", "vocab")),
        P(),
    )
    return jax.shard_map(body, mesh=mesh, in_specs=in_specs, out_specs=out_specs, check_vma=False)
```

profile of v0, /device:TPU:0, one launch (start us, length us, event | category | flops | bytes accessed | tf_op | source)
XLA Modules:
  0.0 1247.0 jit_solution(10427038897527076204)
XLA Ops:
  9.7 64.3 %all-gather.5.cloned.1.call-done = bf16[1,256,7168]{2,1,0:T(8,128)(2,1)} async-done(((bf16[1,8,7168]{2,1,0:T(8,128)(2,1)}), bf16[1,256,7168]{2,1,0:T(8,128)(2,1)}) %all-gather.5.cloned.1.call-update) | async-done | bytes 3670032 | tf_op jit(solution)/shard_map/all_gather | solution.py:50
  76.9 59.1 %all-gather.7.cloned.1.call-done = bf16[1,256,7168]{2,1,0:T(8,128)(2,1)} async-done(((bf16[1,8,7168]{2,1,0:T(8,128)(2,1)}), bf16[1,256,7168]{2,1,0:T(8,128)(2,1)}) %all-gather.7.cloned.1.call-update) | async-done | bytes 3670032 | tf_op jit(solution)/shard_map/all_gather | solution.py:50
  139.0 7.0 fusion.28
  148.5 19.7 %fusion.34 = f32[256,7168]{1,0:T(8,128)} fusion(bf16[576,7168]{1,0:T(8,128)(2,1)} %param.13, bf16[7168,576]{0,1:T(8,128)(2,1)} %param.12, bf16[1,256,7168]{2,1,0:T(8,128)(2,1)} %all-gather.5.cloned.1.call-done, f32[7168]{0:T(1024)S(1)} %copy-done.3, f32[256]{0:T(256)S(1)} %add_rsqrt_fusion.3, f32[256,576]{0,1:T(8,128)S(1)} %fusion.28), kind=kOutput, calls=%fused_computation.41 | convolution fusion | flops 4236083200 | bytes 28144640 | tf_op jit(solution)/shard_map/dot_general | solution.py:56
  168.2 19.3 %fusion.31 = f32[256,7168]{1,0:T(8,128)} fusion(bf16[576,7168]{1,0:T(8,128)(2,1)} %param.13, bf16[7168,576]{0,1:T(8,128)(2,1)} %param.12, bf16[1,256,7168]{2,1,0:T(8,128)(2,1)} %all-gather.7.cloned.1.call-done, f32[256]{0:T(256)S(1)} %add_rsqrt_fusion.1, f32[7168]{0:T(1024)S(1)} %copy-done.3, f32[256,576]{0,1:T(8,128)S(1)} %fusion.25), kind=kOutput, calls=%fused_computation.40 | convolution fusion | flops 4236083200 | bytes 28144640 | tf_op jit(solution)/shard_map/dot_general | solution.py:56
  188.2 251.1 %all-reduce.3.cloned.1.call-done = (f32[256,7168]{1,0:T(8,128)}, f32[256,7168]{1,0:T(8,128)}) async-done(((f32[256,7168]{1,0:T(8,128)}, f32[256,7168]{1,0:T(8,128)}), (f32[256,7168]{1,0:T(8,128)}, f32[256,7168]{1,0:T(8,128)})) %all-reduce.3.cloned.1.call-update) | async-done | bytes 14680080 | tf_op jit(solution)/shard_map/psum | solution.py:55
  439.3 8.4 fusion
  447.7 28.2 %fusion.46 = (f32[256]{0:T(256)S(1)}, f32[256,4040]{0,1:T(8,128)}) fusion(bf16[7168,4040]{0,1:T(8,128)(2,1)} %param.15, f32[7168]{0:T(1024)S(1)} %copy-done.4, f32[256]{0:T(256)S(1)} %add_rsqrt_fusion.2, f32[256,7168]{1,0:T(8,128)} %get-tuple-element.25, bf16[1,256,7168]{2,1,0:T(8,128)(2,1)} %all-gather.5.cloned.1.call-done), kind=kOutput, calls=%fused_computation.75 | convolution fusion | flops 14840743936 | bytes 73095168 | tf_op jit(solution)/shard_map/dot_general | solution.py:60
  476.6 4.8 all-to-all-start.1
  483.6 296.8 %sort.56 = (f32[256,4040]{0,1:T(8,128)}, s32[256,4040]{0,1:T(8,128)}) sort(f32[256,4040]{0,1:T(8,128)} %get-tuple-element.39, s32[256,4040]{0,1:T(8,128)} %iota.24.clone), dimensions={1}, to_apply=%region_18.19 | sort | flops 20684800 | bytes 16547840 | tf_op jit(solution)/shard_map/sort | solution.py:18
  780.4 5.6 copy.39
  786.0 28.4 %fusion.47 = (f32[256]{0:T(256)S(1)}, f32[256,4040]{0,1:T(8,128)}) fusion(bf16[7168,4040]{0,1:T(8,128)(2,1)} %param.15, f32[256]{0:T(256)S(1)} %add_rsqrt_fusion, f32[7168]{0:T(1024)S(1)} %copy-done.4, f32[256,7168]{1,0:T(8,128)} %get-tuple-element.24, bf16[1,256,7168]{2,1,0:T(8,128)(2,1)} %all-gather.7.cloned.1.call-done), kind=kOutput, calls=%fused_computation.76 | convolution fusion | flops 14840743936 | bytes 73095168 | tf_op jit(solution)/shard_map/dot_general | solution.py:60
  814.3 5.1 exponential_reduce_fusion.1
  820.4 296.9 %sort.58 = (f32[256,4040]{0,1:T(8,128)}, s32[256,4040]{0,1:T(8,128)}) sort(f32[256,4040]{0,1:T(8,128)} %get-tuple-element.41, s32[256,4040]{0,1:T(8,128)} %iota.24.clone), dimensions={1}, to_apply=%region_21.22 | sort | flops 20684800 | bytes 16547840 | tf_op jit(solution)/shard_map/sort | solution.py:18
  1117.9 5.5 copy.43
  1123.5 5.9 all-to-all-start.2
  1140.6 7.1 all-to-all-done
  1150.3 7.1 all-to-all-done.4
  1160.0 7.1 all-to-all-done.5
  1169.6 7.1 all-to-all-done.3
  1180.6 40.4 %psum.23 = f32[2,8]{1,0:T(2,128)} all-reduce(f32[2,8]{1,0:T(2,128)S(1)} %pad_maximum_fusion.3), channel_id=1, replica_groups=mesh['section'=2,'vocab'=16] {'section','vocab'}, use_global_device_ids=true, to_apply=%region_26.27 | all-reduce | flops 16 | bytes 128 | tf_op jit(solution)/shard_map/psum | solution.py:94
  1221.0 5.0 all-to-all-start.7
  1227.6 4.9 sort.57
  1234.3 4.9 sort.59
  (81 shorter events, 42.8 us)
Async XLA Ops:
  7.2 131.8 %copy-start.3 = (f32[7168]{0:T(1024)S(1)}, f32[7168]{0:T(1024)}, u32[]{:S(2)}) copy-start(f32[7168]{0:T(1024)} %param.10) | copy-start | bytes 86020
  7.2 66.8 %all-gather.5.cloned.1.call-start = ((), (), s32[]{:S(2)}) async-start(), calls=%async_computation.8 | async-start | bytes 3784704 | tf_op jit(solution)/shard_map/all_gather | solution.py:50
  8.9 127.0 %all-gather.7.cloned.1.call-start = ((), (), s32[]{:S(2)}) async-start(), calls=%async_computation.9 | async-start | bytes 3784704 | tf_op jit(solution)/shard_map/all_gather | solution.py:50
  9.6 429.6 %all-reduce.3.cloned.1.call-start = ((), (), s32[]{:S(2)}) async-start(), calls=%async_computation.10 | async-start | bytes 29360128 | tf_op jit(solution)/shard_map/psum | solution.py:55
  135.9 10.1 slice-start
  138.9 7.1 copy-start
  139.0 7.1 slice-start.1
  187.5 0.7 copy-start.2
  187.5 0.7 copy-start.1
  439.3 8.4 copy-start.4
  476.6 646.9 %all-to-all-start.1 = ((f32[32,1,8]{2,1,0:T(1,128)}), f32[32,1,8]{2,1,0:T(1,128)S(1)}, u32[]{:S(2)}, u32[]{:S(2)}) async-start(f32[32,1,8]{2,1,0:T(1,128)} %bitcast.5), calls=%async_computation.1 | async-start | bytes 32768 | tf_op jit(solution)/shard_map/all_to_all | solution.py:73
  1123.5 13.1 %all-to-all-start.2 = ((f32[32,1,8]{2,1,0:T(1,128)}), f32[32,1,8]{2,1,0:T(1,128)S(1)}, u32[]{:S(2)}, u32[]{:S(2)}) async-start(f32[32,1,8]{2,1,0:T(1,128)} %bitcast.6), calls=%async_computation.2 | async-start | bytes 32768 | tf_op jit(solution)/shard_map/all_to_all | solution.py:76
  1136.6 11.2 all-to-all-start
  1147.8 9.7 all-to-all-start.4
  1157.4 9.6 all-to-all-start.5
  1167.1 9.6 all-to-all-start.3
  1176.7 44.3 %all-to-all-start.6 = ((f32[32,1,160]{2,1,0:T(1,128)}), f32[32,1,160]{2,1,0:T(1,128)S(1)}, u32[]{:S(2)}, u32[]{:S(2)}) async-start(f32[32,1,160]{2,1,0:T(1,128)} %reshape.189), calls=%async_computation.6 | async-start | bytes 65536 | tf_op jit(solution)/shard_map/all_to_all | solution.py:82
  1221.0 12.2 all-to-all-start.7
Sparse Core Ops, SparseCore 0:
  10.8 63.1 all-gather.4
  76.9 59.0 all-gather.6
  187.7 251.5 all-reduce.2
where the time goes:
time: 1260 us; the launch traced here: 1250 us
  other arithmetic  627 us (50%)
  waiting for transfers between devices  406 us (32%)
  matrix products  105 us (8%)
  blocking collectives  40.4 us (3%)
  starting transfers between devices  29.9 us (2%)
  local copies, waits for them, and re-layouts  24.3 us (2%)
  between operations  14.5 us (1%)
    sort x4, other arithmetic, largest(): return lax.sort(values, dimension=values.ndim - 1)[..., -TOPK:]  604 us
    psum x1, waiting for transfers between devices, body(): lax.psum(jnp.dot(hidden_act, w_down, preferred_element_type=jnp.float32),...  251 us
    all_gather x2, waiting for transfers between devices, body(): lax.all_gather(own_rows, ('section', 'vocab'), axis=0, tiled=True)  123 us
    dot_general x2, matrix products, body(): logits = jnp.dot(scaled, head_weight, preferred_element_type=jnp.float32)  56.6 us
    psum x1, blocking collectives, body(): seq_logprob = lax.psum(jnp.stack(partials), ('section', 'vocab'))  40.4 us
    dot_general x2, matrix products, body(): jnp.dot(hidden_act, w_down, preferred_element_type=jnp.float32)  39 us
  transfers between devices with their start and end apart: 11, of which 9 were waited for; matrix products, arithmetic and copies ran while one was open for 53% of the time, Pallas kernels for 0%

commit v1 on v0

--- a/solution.py
+++ b/solution.py
@@ -52,9 +52,8 @@
         gate_proj = jnp.dot(normed, w_gate, preferred_element_type=jnp.float32)
         up_proj = jnp.dot(normed, w_up, preferred_element_type=jnp.float32)
         hidden_act = (jax.nn.silu(gate_proj) * up_proj).astype(jnp.bfloat16)
-        branch = lax.psum(
-            jnp.dot(hidden_act, w_down, preferred_element_type=jnp.float32), ("section", "vocab")
-        )
+        half = lax.psum(jnp.dot(hidden_act, w_down, preferred_element_type=jnp.float32), "section")
+        branch = lax.psum(half, "vocab")
         residual = (gathered.astype(jnp.float32) + branch).astype(jnp.bfloat16)
         scaled = rms_norm(residual, gain_final)
         logits = jnp.dot(scaled, head_weight, preferred_element_type=jnp.float32)

time: 1260 us -> 1470 us (1.17)
  waiting for transfers between devices: 406 us -> 621 us
    psum x0 -> x1, waiting for transfers between devices: none -> 413 us  [body(): branch = lax.psum(half, 'vocab')]
    psum x1, waiting for transfers between devices: 251 us -> 52.2 us  [body(): lax.psum(jnp.dot(hidden_act, w_down, preferred_element_type=jnp.float32),...]
  transfers between devices with their start and end apart: 11 -> 12, of which waited for: 9 -> 10; matrix products, arithmetic and copies ran while one was open for 53% -> 24% of each run, Pallas kernels for 0% -> 0%
where the time goes in v1:
time: 1470 us; the launch traced here: 1460 us
  other arithmetic  627 us (43%)
  waiting for transfers between devices  621 us (42%)
  matrix products  105 us (7%)
  blocking collectives  40.4 us (3%)
  starting transfers between devices  28.7 us (2%)
  local copies, waits for them, and re-layouts  24.3 us (2%)
    sort x4, other arithmetic, largest(): return lax.sort(values, dimension=values.ndim - 1)[..., -TOPK:]  604 us
    psum x1, waiting for transfers between devices, body(): branch = lax.psum(half, 'vocab')  413 us
    all_gather x2, waiting for transfers between devices, body(): lax.all_gather(own_rows, ('section', 'vocab'), axis=0, tiled=True)  123 us
    dot_general x2, matrix products, body(): logits = jnp.dot(scaled, head_weight, preferred_element_type=jnp.float32)  56.4 us
    psum x1, waiting for transfers between devices, body(): lax.psum(jnp.dot(hidden_act, w_down, preferred_element_type=jnp.float32),...  52.2 us
    psum x1, blocking collectives, body(): seq_logprob = lax.psum(jnp.stack(partials), ('section', 'vocab'))  40.4 us
    dot_general x2, matrix products, body(): jnp.dot(hidden_act, w_down, preferred_element_type=jnp.float32)  39 us
  transfers between devices with their start and end apart: 12, of which 10 were waited for; matrix products, arithmetic and copies ran while one was open for 24% of the time, Pallas kernels for 0%

profile of v1, /device:TPU:0, one launch (start us, length us, event | category | flops | bytes accessed | tf_op | source)
XLA Modules:
  0.0 1460.1 jit_solution(1780830453203538435)
XLA Ops:
  9.7 64.3 %all-gather.5.cloned.1.call-done = bf16[1,256,7168]{2,1,0:T(8,128)(2,1)} async-done(((bf16[1,8,7168]{2,1,0:T(8,128)(2,1)}), bf16[1,256,7168]{2,1,0:T(8,128)(2,1)}) %all-gather.5.cloned.1.call-update) | async-done | bytes 3670032 | tf_op jit(solution)/shard_map/all_gather | solution.py:50
  76.9 59.1 %all-gather.7.cloned.1.call-done = bf16[1,256,7168]{2,1,0:T(8,128)(2,1)} async-done(((bf16[1,8,7168]{2,1,0:T(8,128)(2,1)}), bf16[1,256,7168]{2,1,0:T(8,128)(2,1)}) %all-gather.7.cloned.1.call-update) | async-done | bytes 3670032 | tf_op jit(solution)/shard_map/all_gather | solution.py:50
  139.0 7.0 fusion.28
  148.5 19.6 %fusion.34 = f32[256,7168]{1,0:T(8,128)} fusion(bf16[576,7168]{1,0:T(8,128)(2,1)} %param.13, bf16[7168,576]{0,1:T(8,128)(2,1)} %param.12, bf16[1,256,7168]{2,1,0:T(8,128)(2,1)} %all-gather.5.cloned.1.call-done, f32[7168]{0:T(1024)S(1)} %copy-done.3, f32[256]{0:T(256)S(1)} %add_rsqrt_fusion.3, f32[256,576]{0,1:T(8,128)S(1)} %fusion.28), kind=kOutput, calls=%fused_computation.41 | convolution fusion | flops 4236083200 | bytes 28144640 | tf_op jit(solution)/shard_map/dot_general | solution.py:55
  168.1 19.4 %fusion.31 = f32[256,7168]{1,0:T(8,128)} fusion(bf16[576,7168]{1,0:T(8,128)(2,1)} %param.13, bf16[7168,576]{0,1:T(8,128)(2,1)} %param.12, bf16[1,256,7168]{2,1,0:T(8,128)(2,1)} %all-gather.7.cloned.1.call-done, f32[256]{0:T(256)S(1)} %add_rsqrt_fusion.1, f32[7168]{0:T(1024)S(1)} %copy-done.3, f32[256,576]{0,1:T(8,128)S(1)} %fusion.25), kind=kOutput, calls=%fused_computation.40 | convolution fusion | flops 4236083200 | bytes 28144640 | tf_op jit(solution)/shard_map/dot_general | solution.py:55
  188.0 52.2 %all-reduce.7.cloned.1.call-done = (f32[256,7168]{1,0:T(8,128)}, f32[256,7168]{1,0:T(8,128)}) async-done(((f32[256,7168]{1,0:T(8,128)}, f32[256,7168]{1,0:T(8,128)}), (f32[256,7168]{1,0:T(8,128)}, f32[256,7168]{1,0:T(8,128)})) %all-reduce.7.cloned.1.call-update) | async-done | bytes 14680080 | tf_op jit(solution)/shard_map/psum | solution.py:55
  240.9 413.4 %all-reduce.5.cloned.1.call-done = (f32[256,7168]{1,0:T(8,128)}, f32[256,7168]{1,0:T(8,128)}) async-done(((f32[256,7168]{1,0:T(8,128)}, f32[256,7168]{1,0:T(8,128)}), (f32[256,7168]{1,0:T(8,128)}, f32[256,7168]{1,0:T(8,128)})) %all-reduce.5.cloned.1.call-update) | async-done | bytes 14680080 | tf_op jit(solution)/shard_map/psum | solution.py:56
  654.3 8.4 fusion
  662.7 28.2 %fusion.46 = (f32[256]{0:T(256)S(1)}, f32[256,4040]{0,1:T(8,128)}) fusion(bf16[7168,4040]{0,1:T(8,128)(2,1)} %param.15, f32[7168]{0:T(1024)S(1)} %copy-done.4, f32[256]{0:T(256)S(1)} %add_rsqrt_fusion.2, f32[256,7168]{1,0:T(8,128)} %get-tuple-element.25, bf16[1,256,7168]{2,1,0:T(8,128)(2,1)} %all-gather.5.cloned.1.call-done), kind=kOutput, calls=%fused_computation.75 | convolution fusion | flops 14840743936 | bytes 73095168 | tf_op jit(solution)/shard_map/dot_general | solution.py:59
  693.1 296.8 %sort.56 = (f32[256,4040]{0,1:T(8,128)}, s32[256,4040]{0,1:T(8,128)}) sort(f32[256,4040]{0,1:T(8,128)} %get-tuple-element.41, s32[256,4040]{0,1:T(8,128)} %iota.24.clone), dimensions={1}, to_apply=%region_20.21 | sort | flops 20684800 | bytes 16547840 | tf_op jit(solution)/shard_map/sort | solution.py:18
  990.0 5.6 copy.39
  999.5 28.2 %fusion.47 = (f32[256]{0:T(256)S(1)}, f32[256,4040]{0,1:T(8,128)}) fusion(bf16[7168,4040]{0,1:T(8,128)(2,1)} %param.15, f32[256]{0:T(256)S(1)} %add_rsqrt_fusion, f32[7168]{0:T(1024)S(1)} %copy-done.4, f32[256,7168]{1,0:T(8,128)} %get-tuple-element.24, bf16[1,256,7168]{2,1,0:T(8,128)(2,1)} %all-gather.7.cloned.1.call-done), kind=kOutput, calls=%fused_computation.76 | convolution fusion | flops 14840743936 | bytes 73095168 | tf_op jit(solution)/shard_map/dot_general | solution.py:59
  1027.7 5.1 exponential_reduce_fusion.1
  1033.7 296.8 %sort.58 = (f32[256,4040]{0,1:T(8,128)}, s32[256,4040]{0,1:T(8,128)}) sort(f32[256,4040]{0,1:T(8,128)} %get-tuple-element.43, s32[256,4040]{0,1:T(8,128)} %iota.24.clone), dimensions={1}, to_apply=%region_23.24 | sort | flops 20684800 | bytes 16547840 | tf_op jit(solution)/shard_map/sort | solution.py:18
  1331.2 5.5 copy.43
  1336.8 5.8 all-to-all-start.2
  1353.8 7.1 all-to-all-done
  1363.5 7.1 all-to-all-done.4
  1373.2 7.1 all-to-all-done.5
  1382.8 7.1 all-to-all-done.3
  1393.8 40.4 %psum.39 = f32[2,8]{1,0:T(2,128)} all-reduce(f32[2,8]{1,0:T(2,128)S(1)} %pad_maximum_fusion.3), channel_id=1, replica_groups=mesh['section'=2,'vocab'=16] {'section','vocab'}, use_global_device_ids=true, to_apply=%region_28.29 | all-reduce | flops 16 | bytes 128 | tf_op jit(solution)/shard_map/psum | solution.py:93
  1434.2 5.0 all-to-all-start.7
  1440.7 4.9 sort.57
  1447.4 4.9 sort.59
  (84 shorter events, 46.6 us)
Async XLA Ops:
  7.2 131.8 %copy-start.3 = (f32[7168]{0:T(1024)S(1)}, f32[7168]{0:T(1024)}, u32[]{:S(2)}) copy-start(f32[7168]{0:T(1024)} %param.10) | copy-start | bytes 86020
  7.2 66.8 %all-gather.5.cloned.1.call-start = ((), (), s32[]{:S(2)}) async-start(), calls=%async_computation.8 | async-start | bytes 3784704 | tf_op jit(solution)/shard_map/all_gather | solution.py:50
  8.9 127.0 %all-gather.7.cloned.1.call-start = ((), (), s32[]{:S(2)}) async-start(), calls=%async_computation.9 | async-start | bytes 3784704 | tf_op jit(solution)/shard_map/all_gather | solution.py:50
  9.6 230.6 %all-reduce.7.cloned.1.call-start = ((), (), s32[]{:S(2)}) async-start(), calls=%async_computation.11 | async-start | bytes 29360128 | tf_op jit(solution)/shard_map/psum | solution.py:55
  135.9 10.1 slice-start
  138.9 7.1 copy-start
  139.0 7.1 slice-start.1
  187.5 466.8 %all-reduce.5.cloned.1.call-start = ((), (), s32[]{:S(2)}) async-start(), calls=%async_computation.10 | async-start | bytes 29360128 | tf_op jit(solution)/shard_map/psum | solution.py:56
  240.2 0.7 copy-start.2
  240.2 0.7 copy-start.1
  654.3 8.4 copy-start.4
  996.2 340.5 %all-to-all-start.1 = ((f32[32,1,8]{2,1,0:T(1,128)}), f32[32,1,8]{2,1,0:T(1,128)S(1)}, u32[]{:S(2)}, u32[]{:S(2)}) async-start(f32[32,1,8]{2,1,0:T(1,128)} %bitcast.5), calls=%async_computation.1 | async-start | bytes 32768 | tf_op jit(solution)/shard_map/all_to_all | solution.py:72
  1336.8 13.0 all-to-all-start.2
  1349.8 11.2 all-to-all-start
  1360.9 9.7 all-to-all-start.4
  1370.6 9.6 all-to-all-start.5
  1380.3 9.6 all-to-all-start.3
  1389.9 44.3 %all-to-all-start.6 = ((f32[32,1,160]{2,1,0:T(1,128)}), f32[32,1,160]{2,1,0:T(1,128)S(1)}, u32[]{:S(2)}, u32[]{:S(2)}) async-start(f32[32,1,160]{2,1,0:T(1,128)} %reshape.189), calls=%async_computation.6 | async-start | bytes 65536 | tf_op jit(solution)/shard_map/all_to_all | solution.py:81
  1434.2 12.2 all-to-all-start.7
Sparse Core Ops, SparseCore 0:
  10.8 63.1 all-gather.4
  76.9 59.0 all-gather.6
  187.6 52.5 all-reduce.6
  246.5 407.7 all-reduce.4
